TPU v7x, 32 devices: a whole 2x2x4 slice. The times are simulated.
32 devices in a mesh: row: 8 (over y, x, core), col: 4 (over z).
Axes of the slice: x: 2, y: 2, z: 4, core: 2. Of those that a mesh axis runs over, the one named last changes fastest.
Arguments:
- density: float32 [256, 256, 256], P('row', 'col'), may hold values from -5 to 5
- green_octant: float32 [256, 256, 256], P('row', 'col'), may hold values from 0 to 0.25
Outputs:
- potential: float32 [256, 256, 256], P('row', 'col')
All inputs are finite; a program needn't handle non-finite values.
Results may differ from a plain program's by a relative error of at most 0.000092.
Values sent between devices are 32-bit elements; how exact they have to be, the bound alone decides.
A program may use at most 192 MiB of HBM per device.

v0:
```python
import jax
import jax.numpy as jnp
from jax import lax
from jax.sharding import PartitionSpec as P


def tables(extent, padded):
    positions = lax.iota(jnp.int32, extent)[:, None]
    waves = lax.iota(jnp.int32, padded)[None, :]
    phases = positions * waves % padded
    angles = phases.astype(jnp.float32) * jnp.float32(2.0 * 3.141592653589793 / padded)
    weights = jnp.where(positions == 0, jnp.float32(1.0), jnp.float32(2.0))
    cosine = jnp.cos(angles)
    return (cosine, jnp.sin(angles), weights * cosine)


def contract(pattern, operand, matrix):
    return jnp.einsum(
        pattern,
        operand,
        matrix,
        precision=lax.Precision.HIGHEST,
        preferred_element_type=jnp.float32,
    )


def forward(pattern, real_part, imaginary, kernel, cosine, sine_table, kernel_table):
    new_real = contract(pattern, real_part, cosine) + contract(pattern, imaginary, sine_table)
    new_imaginary = contract(pattern, imaginary, cosine) - contract(pattern, real_part, sine_table)
    return (new_real, new_imaginary, contract(pattern, kernel, kernel_table))


def inverse(pattern, real_part, imaginary, cosine, sine_table):
    new_real = contract(pattern, real_part, cosine) - contract(pattern, imaginary, sine_table)
    new_imaginary = contract(pattern, imaginary, cosine) + contract(pattern, real_part, sine_table)
    return (new_real, new_imaginary)


def nyquist_plane(density, green_octant, cosine, sine_table, kernel_table):
    extent = density.shape[2]
    local_cols = density.shape[1]
    alternating = cosine[:, extent]
    dens_line = contract("xyz,z->xy", density, alternating)
    kern_line = contract("xyz,z->xy", green_octant, kernel_table[:, extent])
    dens_line, kern_line = (
        lax.all_gather(dens_line, "col", axis=1, tiled=True),
        lax.all_gather(kern_line, "col", axis=1, tiled=True),
    )
    real_part = contract("xy,yq->xq", dens_line, cosine)
    imaginary = -contract("xy,yq->xq", dens_line, sine_table)
    kernel = contract("xy,yq->xq", kern_line, kernel_table)
    real_part, imaginary, kernel = (
        lax.all_to_all(real_part, "row", split_axis=1, concat_axis=0, tiled=True),
        lax.all_to_all(imaginary, "row", split_axis=1, concat_axis=0, tiled=True),
        lax.all_to_all(kernel, "row", split_axis=1, concat_axis=0, tiled=True),
    )
    real_part, imaginary, kernel = forward(
        "xq,xp->pq", real_part, imaginary, kernel, cosine, sine_table, kernel_table
    )
    real_part = real_part * kernel
    imaginary = imaginary * kernel
    real_part, imaginary = inverse("pq,xp->xq", real_part, imaginary, cosine, sine_table)
    real_part, imaginary = (
        lax.all_to_all(real_part, "row", split_axis=0, concat_axis=1, tiled=True),
        lax.all_to_all(imaginary, "row", split_axis=0, concat_axis=1, tiled=True),
    )
    whole = contract("xq,yq->xy", real_part, cosine) - contract("xq,yq->xy", imaginary, sine_table)
    start = lax.axis_index("col") * local_cols
    return lax.dynamic_slice_in_dim(whole, start, local_cols, 1)


def on_device(density, green_octant):
    extent = density.shape[2]
    padded = 2 * extent
    cosine, sine_table, kernel_table = tables(extent, padded)
    half_cos = cosine[:, :extent]
    half_sin = sine_table[:, :extent]
    real_part = contract("xyz,zk->xyk", density, half_cos)
    imaginary = -contract("xyz,zk->xyk", density, half_sin)
    kernel = contract("xyz,zk->xyk", green_octant, kernel_table[:, :extent])
    real_part, imaginary, kernel = (
        lax.all_to_all(real_part, "col", split_axis=2, concat_axis=1, tiled=True),
        lax.all_to_all(imaginary, "col", split_axis=2, concat_axis=1, tiled=True),
        lax.all_to_all(kernel, "col", split_axis=2, concat_axis=1, tiled=True),
    )
    real_part, imaginary, kernel = forward(
        "xyk,yq->xqk", real_part, imaginary, kernel, cosine, sine_table, kernel_table
    )
    real_part, imaginary, kernel = (
        lax.all_to_all(real_part, "row", split_axis=1, concat_axis=0, tiled=True),
        lax.all_to_all(imaginary, "row", split_axis=1, concat_axis=0, tiled=True),
        lax.all_to_all(kernel, "row", split_axis=1, concat_axis=0, tiled=True),
    )
    real_part, imaginary, kernel = forward(
        "xqk,xp->pqk", real_part, imaginary, kernel, cosine, sine_table, kernel_table
    )
    real_part = real_part * kernel
    imaginary = imaginary * kernel
    real_part, imaginary = inverse("pqk,xp->xqk", real_part, imaginary, cosine, sine_table)
    real_part, imaginary = (
        lax.all_to_all(real_part, "row", split_axis=0, concat_axis=1, tiled=True),
        lax.all_to_all(imaginary, "row", split_axis=0, concat_axis=1, tiled=True),
    )
    real_part, imaginary = inverse("xqk,yq->xyk", real_part, imaginary, cosine, sine_table)
    real_part, imaginary = (
        lax.all_to_all(real_part, "col", split_axis=1, concat_axis=2, tiled=True),
        lax.all_to_all(imaginary, "col", split_axis=1, concat_axis=2, tiled=True),
    )
    highest = nyquist_plane(density, green_octant, cosine, sine_table, kernel_table)
    waves = lax.iota(jnp.int32, extent)[None, :]
    doubling = jnp.where(waves == 0, jnp.float32(1.0), jnp.float32(2.0))
    summed = contract("xyk,zk->xyz", real_part, half_cos * doubling) - contract(
        "xyk,zk->xyz", imaginary, half_sin * doubling
    )
    summed = summed + highest[:, :, None] * cosine[:, extent][None, None, :]
    scaling = 1.0 / float(padded * padded * padded)
    return summed * jnp.float32(scaling)


def solution(mesh):
    return jax.shard_map(
        on_device,
        mesh=mesh,
        in_specs=(P("row", "col", None), P("row", "col", None)),
        out_specs=P("row", "col", None),
        check_vma=False,
    )
```

profile of v0, /device:TPU:0, one launch (start us, length us, event | category | flops | bytes accessed | tf_op | source)
XLA Modules:
  0.0 1007.9 jit_solution(2282553187442278310)
XLA Ops:
  39.4 32.2 %all-to-all-done.1 = f32[4,1,131072]{2,1,0:T(1,128)} async-done(((f32[4,1,131072]{2,1,0:T(1,128)}), f32[4,1,131072]{2,1,0:T(1,128)}, u32[]{:S(2)}, u32[]{:S(2)}) %all-to-all-start.1) | async-done | bytes 2097184 | tf_op jit(solution)/shard_map/all_to_all | solution.py:83
  94.0 30.1 %all-to-all-done = f32[4,1,131072]{2,1,0:T(1,128)} async-done(((f32[4,1,131072]{2,1,0:T(1,128)}), f32[4,1,131072]{2,1,0:T(1,128)}, u32[]{:S(2)}, u32[]{:S(2)}) %all-to-all-start) | async-done | bytes 2097184 | tf_op jit(solution)/shard_map/all_to_all | solution.py:82
  129.1 9.0 reduce.7
  150.5 13.8 %all_to_all.207 = f32[32,256,64]{1,2,0:T(8,128)} reshape(f32[32,4,64,64]{2,1,3,0:T(4,128)} %bitcast.280) | data formatting | bytes 4194304 | tf_op jit(solution)/shard_map/all_to_all | solution.py:83
  164.3 9.0 reduce.8
  207.7 9.1 copy.41
  216.8 9.8 reshape.93
  247.6 9.1 copy.44
  256.7 9.8 reshape.95
  266.6 13.7 %all-to-all-done.2 = f32[8,1,131072]{2,1,0:T(1,128)} async-done(((f32[8,1,131072]{2,1,0:T(1,128)}), f32[8,1,131072]{2,1,0:T(1,128)}, u32[]{:S(2)}, u32[]{:S(2)}) %all-to-all-start.2) | async-done | bytes 4194336 | tf_op jit(solution)/shard_map/all_to_all | solution.py:90
  284.9 9.0 reduce.5
  311.9 8.6 fusion.71
  320.5 9.1 copy.49
  329.6 9.8 reshape.87
  346.7 13.8 %all-gather = f32[4,64,32]{1,2,0:T(8,128)S(1)} all-gather(f32[1,64,32]{1,2,0:T(8,128)S(1)} %bitcast.308), channel_id=1, replica_groups=mesh['row'=8,'col'=4] {'col'}, dimensions={0}, use_global_device_ids=true | all-gather | bytes 40960 | tf_op jit(solution)/shard_map/all_gather | solution.py:46
  370.2 13.2 %all-gather.1 = f32[4,64,32]{1,2,0:T(8,128)S(1)} all-gather(f32[1,64,32]{1,2,0:T(8,128)S(1)} %bitcast.307), channel_id=1, replica_groups=mesh['row'=8,'col'=4] {'col'}, dimensions={0}, use_global_device_ids=true | all-gather | bytes 40960 | tf_op jit(solution)/shard_map/all_gather | solution.py:47
  386.8 13.9 %reduce.10 = f32[8,131072]{1,0:T(8,128)} reduce(f32[8,1,131072]{2,1,0:T(1,128)} %all-to-all-done.2, f32[]{:T(128)} %broadcast.80), dimensions={1}, to_apply=%all_to_all.208.reduce_sub_computation | reduce | bytes 8388612 | tf_op jit(solution)/shard_map/all_to_all | solution.py:90
  400.7 8.7 reshape.94
  409.3 11.3 %copy.42 = f32[32,8,64,64]{3,2,0,1:T(8,128)} copy(f32[32,8,64,64]{3,0,2,1:T(8,128)} %bitcast.253) | data formatting | bytes 8388608 | tf_op jit(solution)/shard_map/all_to_all | solution.py:90
  428.4 14.1 %reduce.9 = f32[8,131072]{1,0:T(8,128)} reduce(f32[8,1,131072]{2,1,0:T(1,128)} %all-to-all-done.3, f32[]{:T(128)} %broadcast.80), dimensions={1}, to_apply=%all_to_all.212.reduce_sub_computation | reduce | bytes 8388612 | tf_op jit(solution)/shard_map/all_to_all | solution.py:91
  442.5 8.7 reshape.96
  451.2 11.3 %copy.45 = f32[32,8,64,64]{3,2,0,1:T(8,128)} copy(f32[32,8,64,64]{3,0,2,1:T(8,128)} %bitcast.255) | data formatting | bytes 8388608 | tf_op jit(solution)/shard_map/all_to_all | solution.py:91
  470.3 14.8 %fusion.35 = f32[512,4096]{0,1} fusion(f32[256,4096]{0,1:T(8,128)} %bitcast.239), kind=kOutput, calls=%fused_computation.51 | convolution fusion | flops 6444285952 | bytes 12582912
  485.1 13.0 %fusion.62 = f32[512,4096]{0,1} fusion(f32[256,4096]{0,1:T(8,128)S(1)} %bitcast.240), kind=kOutput, calls=%fused_computation.62 | convolution fusion | flops 6444285952 | bytes 12582912
  498.1 13.2 %fusion.60 = f32[512,4096]{0,1} fusion(f32[256,4096]{0,1:T(8,128)S(1)} %bitcast.237), kind=kOutput, calls=%fused_computation.61 | convolution fusion | flops 6444285952 | bytes 12582912
  511.2 12.9 %fusion.41 = f32[512,4096]{0,1} fusion(f32[256,4096]{0,1:T(8,128)S(1)} %bitcast.238), kind=kOutput, calls=%fused_computation.54 | convolution fusion | flops 6444285952 | bytes 12582912
  528.7 13.6 %reduce.6 = f32[8,131072]{1,0:T(8,128)} reduce(f32[8,1,131072]{2,1,0:T(1,128)} %all-to-all-done.5, f32[]{:T(128)} %broadcast.80), dimensions={1}, to_apply=%all_to_all.220.reduce_sub_computation | reduce | bytes 8388612 | tf_op jit(solution)/shard_map/all_to_all | solution.py:92
  542.4 8.7 reshape.88
  551.0 11.3 %copy.50 = f32[32,8,64,64]{3,2,0,1:T(8,128)} copy(f32[32,8,64,64]{3,0,2,1:T(8,128)} %bitcast.257) | data formatting | bytes 8388608 | tf_op jit(solution)/shard_map/all_to_all | solution.py:92
  570.1 14.6 %fusion.70 = f32[512,4096]{0,1} fusion(f32[256,4096]{0,1:T(8,128)} %bitcast.270, f32[256]{0:T(256)S(1)} %compare_select_fusion), kind=kOutput, calls=%fused_computation.67 | convolution fusion | flops 6444417024 | bytes 12583936
  584.7 22.7 %subtract_multiply_fusion = (f32[512,64,64]{0,2,1:T(8,128)}, f32[512,64,64]{0,2,1:T(8,128)}) fusion(f32[512,64,64]{0,2,1:T(8,128)} %bitcast.249, f32[512,64,64]{0,2,1:T(8,128)} %bitcast.245, f32[512,64,64]{0,2,1:T(8,128)} %bitcast.247, f32[512,64,64]{0,2,1:T(8,128)} %bitcast.248, f32[512,64,64]{0,2,1:T(8,128)} %bitcast.246), kind=kLoop, calls=%fused_computation | loop fusion | flops 8388608 | bytes 58720256 | tf_op jit(solution)/shard_map/mul | solution.py:98
  611.6 14.1 %fusion.56 = f32[256,4096]{0,1} fusion(f32[512,4096]{0,1:T(8,128)} %bitcast.235), kind=kOutput, calls=%fused_computation.59 | convolution fusion | flops 6444285952 | bytes 12582912
  630.1 13.6 %fusion.31 = f32[256,4096]{0,1:S(1)} fusion(f32[512,4096]{0,1:T(8,128)} %bitcast.233), kind=kOutput, calls=%fused_computation.49 | convolution fusion | flops 6444285952 | bytes 12582912
  646.6 9.1 copy.56
  655.7 9.8 reshape.99
  670.6 13.4 %fusion.37 = f32[256,4096]{0,1:S(1)} fusion(f32[512,4096]{0,1:T(8,128)} %bitcast.236), kind=kOutput, calls=%fused_computation.52 | convolution fusion | flops 6444285952 | bytes 12582912
  684.0 13.3 %fusion.58 = f32[256,4096]{0,1:S(1)} fusion(f32[512,4096]{0,1:T(8,128)} %bitcast.234), kind=kOutput, calls=%fused_computation.60 | convolution fusion | flops 6444285952 | bytes 12582912
  700.1 9.3 copy.54
  709.4 9.8 reshape.97
  751.6 14.1 %reduce.12 = f32[8,131072]{1,0:T(8,128)} reduce(f32[8,1,131072]{2,1,0:T(1,128)} %all-to-all-done.7, f32[]{:T(128)} %broadcast.80), dimensions={1}, to_apply=%all_to_all.228.reduce_sub_computation | reduce | bytes 8388612 | tf_op jit(solution)/shard_map/all_to_all | solution.py:102
  765.8 8.7 reshape.100
  774.4 9.3 copy.57
  803.1 13.7 %reduce.11 = f32[8,131072]{1,0:T(8,128)} reduce(f32[8,1,131072]{2,1,0:T(1,128)} %all-to-all-done.6, f32[]{:T(128)} %broadcast.80), dimensions={1}, to_apply=%all_to_all.224.reduce_sub_computation | reduce | bytes 8388612 | tf_op jit(solution)/shard_map/all_to_all | solution.py:101
  816.8 8.7 reshape.98
  825.5 9.3 copy.55
  842.2 8.8 fusion.52
  900.7 23.0 %all-to-all-done.9 = f32[4,1,131072]{2,1,0:T(1,128)} async-done(((f32[4,1,131072]{2,1,0:T(1,128)}), f32[4,1,131072]{2,1,0:T(1,128)}, u32[]{:S(2)}, u32[]{:S(2)}) %all-to-all-start.9) | async-done | bytes 2097184 | tf_op jit(solution)/shard_map/all_to_all | solution.py:107
  959.5 16.9 %all-to-all-done.8 = f32[4,1,131072]{2,1,0:T(1,128)} async-done(((f32[4,1,131072]{2,1,0:T(1,128)}), f32[4,1,131072]{2,1,0:T(1,128)}, u32[]{:S(2)}, u32[]{:S(2)}) %all-to-all-start.8) | async-done | bytes 2097184 | tf_op jit(solution)/shard_map/all_to_all | solution.py:106
  (161 shorter events, 400.0 us)
Async XLA Ops:
  0.0 2.7 copy-start
  1.9 0.8 copy-start.12
  16.9 54.6 %all-to-all-start.1 = ((f32[4,1,131072]{2,1,0:T(1,128)}), f32[4,1,131072]{2,1,0:T(1,128)}, u32[]{:S(2)}, u32[]{:S(2)}) async-start(f32[4,1,131072]{2,1,0:T(1,128)} %reshape.91), calls=%async_computation.1 | async-start | bytes 4194304 | tf_op jit(solution)/shard_map/all_to_all | solution.py:83
  25.2 318.8 %copy-start.10 = (f32[256,512]{1,0:T(8,128)}, f32[256,512]{1,0:T(8,128)S(1)}, u32[]{:S(2)}) copy-start(f32[256,512]{1,0:T(8,128)S(1)} %fusion.16) | copy-start | bytes 1572868
  71.6 52.6 %all-to-all-start = ((f32[4,1,131072]{2,1,0:T(1,128)}), f32[4,1,131072]{2,1,0:T(1,128)}, u32[]{:S(2)}, u32[]{:S(2)}) async-start(f32[4,1,131072]{2,1,0:T(1,128)} %reshape.89), calls=%async_computation | async-start | bytes 4194304 | tf_op jit(solution)/shard_map/all_to_all | solution.py:82
  124.1 102.5 %all-to-all-start.4 = ((f32[4,1,131072]{2,1,0:T(1,128)}), f32[4,1,131072]{2,1,0:T(1,128)}, u32[]{:S(2)}, u32[]{:S(2)}) async-start(f32[4,1,131072]{2,1,0:T(1,128)} %reshape.85), calls=%async_computation.4 | async-start | bytes 4194304 | tf_op jit(solution)/shard_map/all_to_all | solution.py:84
  191.3 7.4 copy-start.5
  226.6 53.7 %all-to-all-start.2 = ((f32[8,1,131072]{2,1,0:T(1,128)}), f32[8,1,131072]{2,1,0:T(1,128)}, u32[]{:S(2)}, u32[]{:S(2)}) async-start(f32[8,1,131072]{2,1,0:T(1,128)} %reshape.93), calls=%async_computation.2 | async-start | bytes 8388608 | tf_op jit(solution)/shard_map/all_to_all | solution.py:90
  231.2 7.5 copy-start.6
  280.3 59.1 %all-to-all-start.3 = ((f32[8,1,131072]{2,1,0:T(1,128)}), f32[8,1,131072]{2,1,0:T(1,128)}, u32[]{:S(2)}, u32[]{:S(2)}) async-start(f32[8,1,131072]{2,1,0:T(1,128)} %reshape.95), calls=%async_computation.3 | async-start | bytes 8388608 | tf_op jit(solution)/shard_map/all_to_all | solution.py:91
  339.4 184.7 %all-to-all-start.5 = ((f32[8,1,131072]{2,1,0:T(1,128)}), f32[8,1,131072]{2,1,0:T(1,128)}, u32[]{:S(2)}, u32[]{:S(2)}) async-start(f32[8,1,131072]{2,1,0:T(1,128)} %reshape.87), calls=%async_computation.5 | async-start | bytes 8388608 | tf_op jit(solution)/shard_map/all_to_all | solution.py:92
  344.1 16.4 %copy-start.14 = (f32[256]{0:T(256)}, f32[256]{0:T(256)S(1)}, u32[]{:S(2)}) copy-start(f32[256]{0:T(256)S(1)} %slice_reduce_fusion.1) | copy-start | bytes 3076
  346.7 20.9 %copy-start.9 = (f32[32,64,256]{2,1,0:T(8,128)S(1)}, f32[32,64,256]{2,1,0:T(8,128)}, u32[]{:S(2)}) copy-start(f32[32,64,256]{2,1,0:T(8,128)} %param.3) | copy-start | bytes 6291460
  470.3 14.8 %copy-start.3 = (f32[256,64,64]{0,2,1:T(8,128)S(1)}, f32[256,64,64]{0,2,1:T(8,128)}, u32[]{:S(2)}) copy-start(f32[256,64,64]{0,2,1:T(8,128)} %copy.46) | copy-start | bytes 12582916
  485.1 13.0 %copy-start.2 = (f32[256,64,64]{0,2,1:T(8,128)S(1)}, f32[256,64,64]{0,2,1:T(8,128)}, u32[]{:S(2)}) copy-start(f32[256,64,64]{0,2,1:T(8,128)} %copy.43) | copy-start | bytes 12582916
  524.1 83.2 %all-to-all-start.11 = ((f32[8,1,2048]{2,1,0:T(1,128)}), f32[8,1,2048]{2,1,0:T(1,128)S(1)}, u32[]{:S(2)}, u32[]{:S(2)}) async-start(f32[8,1,2048]{2,1,0:T(1,128)} %reshape.107), calls=%async_computation.11 | async-start | bytes 131072 | tf_op jit(solution)/shard_map/all_to_all | solution.py:54
  607.4 18.3 %all-to-all-start.10 = ((f32[8,1,2048]{2,1,0:T(1,128)}), f32[8,1,2048]{2,1,0:T(1,128)S(1)}, u32[]{:S(2)}, u32[]{:S(2)}) async-start(f32[8,1,2048]{2,1,0:T(1,128)} %reshape.109), calls=%async_computation.10 | async-start | bytes 131072 | tf_op jit(solution)/shard_map/all_to_all | solution.py:53
  625.7 39.9 %all-to-all-start.12 = ((f32[8,1,2048]{2,1,0:T(1,128)}), f32[8,1,2048]{2,1,0:T(1,128)S(1)}, u32[]{:S(2)}, u32[]{:S(2)}) async-start(f32[8,1,2048]{2,1,0:T(1,128)} %reshape.105), calls=%async_computation.12 | async-start | bytes 131072 | tf_op jit(solution)/shard_map/all_to_all | solution.py:55
  630.1 13.6 %copy-start.7 = (f32[256,4096]{0,1:S(1)}, f32[256,4096]{0,1}, u32[]{:S(2)}) copy-start(f32[256,4096]{0,1} %fusion.56) | copy-start | bytes 12582916
  665.6 54.1 %all-to-all-start.7 = ((f32[8,1,131072]{2,1,0:T(1,128)}), f32[8,1,131072]{2,1,0:T(1,128)}, u32[]{:S(2)}, u32[]{:S(2)}) async-start(f32[8,1,131072]{2,1,0:T(1,128)} %reshape.99), calls=%async_computation.7 | async-start | bytes 8388608 | tf_op jit(solution)/shard_map/all_to_all | solution.py:102
  719.7 79.1 %all-to-all-start.6 = ((f32[8,1,131072]{2,1,0:T(1,128)}), f32[8,1,131072]{2,1,0:T(1,128)}, u32[]{:S(2)}, u32[]{:S(2)}) async-start(f32[8,1,131072]{2,1,0:T(1,128)} %reshape.97), calls=%async_computation.6 | async-start | bytes 8388608 | tf_op jit(solution)/shard_map/all_to_all | solution.py:101
  798.7 52.3 %all-to-all-start.14 = ((f32[8,1,2048]{2,1,0:T(1,128)}), f32[8,1,2048]{2,1,0:T(1,128)S(1)}, u32[]{:S(2)}, u32[]{:S(2)}) async-start(f32[8,1,2048]{2,1,0:T(1,128)} %reshape.111), calls=%async_computation.14 | async-start | bytes 131072 | tf_op jit(solution)/shard_map/all_to_all | solution.py:65
  851.0 19.0 %all-to-all-start.13 = ((f32[8,1,2048]{2,1,0:T(1,128)}), f32[8,1,2048]{2,1,0:T(1,128)S(1)}, u32[]{:S(2)}, u32[]{:S(2)}) async-start(f32[8,1,2048]{2,1,0:T(1,128)} %reshape.113), calls=%async_computation.13 | async-start | bytes 131072 | tf_op jit(solution)/shard_map/all_to_all | solution.py:64
  870.0 53.7 %all-to-all-start.9 = ((f32[4,1,131072]{2,1,0:T(1,128)}), f32[4,1,131072]{2,1,0:T(1,128)}, u32[]{:S(2)}, u32[]{:S(2)}) async-start(f32[4,1,131072]{2,1,0:T(1,128)} %reshape.103), calls=%async_computation.9 | async-start | bytes 4194304 | tf_op jit(solution)/shard_map/all_to_all | solution.py:107
  874.5 7.6 copy-start.4
  923.7 52.8 %all-to-all-start.8 = ((f32[4,1,131072]{2,1,0:T(1,128)}), f32[4,1,131072]{2,1,0:T(1,128)}, u32[]{:S(2)}, u32[]{:S(2)}) async-start(f32[4,1,131072]{2,1,0:T(1,128)} %reshape.101), calls=%async_computation.8 | async-start | bytes 4194304 | tf_op jit(solution)/shard_map/all_to_all | solution.py:106
  994.9 5.6 copy-start.11
  994.9 9.3 copy-start.13
  994.9 9.3 copy-start.15
  1000.5 3.7 copy-start.8
  1000.5 7.0 copy-start.1
where the time goes:
time: 1020 us; the launch traced here: 1010 us
  local copies, waits for them, and re-layouts  386 us (38%)
  matrix products  246 us (24%)
  other arithmetic  162 us (16%)
  waiting for transfers between devices  116 us (11%)
  starting transfers between devices  70 us (7%)
  blocking collectives  27 us (3%)
    unnamed x18, matrix products  187 us
    unnamed x64, local copies, waits for them, and re-layouts  150 us
    dot_general x21, matrix products, contract(): jnp.einsum(pattern, operand, matrix, precision=lax.Precision.HIGHEST, pre...  58.8 us
    all_to_all x1, waiting for transfers between devices, on_device(): lax.all_to_all(imaginary, 'col', split_axis=2, concat_axis=1, tiled=True)  32.2 us
    all_to_all x1, waiting for transfers between devices, on_device(): lax.all_to_all(real_part, 'col', split_axis=2, concat_axis=1, tiled=True)  30.1 us
    all_to_all x1, waiting for transfers between devices, on_device(): lax.all_to_all(imaginary, 'col', split_axis=1, concat_axis=2, tiled=True)  23 us
    mul x1, other arithmetic, on_device(): imaginary = imaginary * kernel  22.7 us
    all_to_all x2, local copies, waits for them, and re-layouts, on_device(): lax.all_to_all(imaginary, 'col', split_axis=2, concat_axis=1, tiled=True)  20.7 us
  transfers between devices with their start and end apart: 15, of which 6 were waited for; matrix products, arithmetic and copies ran while one was open for 69% of the time, Pallas kernels for 0%

commit v1 on v0

v1 whole, which is shorter than its diff:
```python
import jax
import jax.numpy as jnp
import numpy as np
from jax import lax
from jax.experimental import pallas as pl
from jax.experimental.pallas import tpu as pltpu
from jax.sharding import PartitionSpec as P

F32 = jnp.float32
BF16 = jnp.bfloat16
VMEM_BYTES = 60 * 1024 * 1024


def trig(extent):
    k = np.arange(extent)[:, None]
    n = np.arange(extent)[None, :]
    phase = ((2 * k + 1) * n) % (4 * extent)
    angle = 2.0 * np.pi * phase / (4 * extent)
    weight = np.where(n == 0, 1.0, 2.0)
    return np.cos(angle), np.sin(angle), weight * np.cos(angle)


def halves(table):
    table = np.asarray(table, np.float32)
    high = table.astype(BF16)
    low = (table - high.astype(np.float32)).astype(BF16)
    return jnp.asarray(np.stack([high, low]))


def split(value):
    high = value.astype(BF16)
    return high, (value - high.astype(F32)).astype(BF16)


def dot3(left, right, dims=((1,), (0,))):
    def one(a, b):
        return lax.dot_general(a, b, (dims, ((), ())), preferred_element_type=F32)

    return one(left[0], right[0]) + (one(left[0], right[1]) + one(left[1], right[0]))


def forward_z_kernel(groups, dens_ref, green_ref, wave_ref, even_ref, dens_out, green_out):
    step = pl.program_id(0)
    tiles = dens_ref.shape[0] // 128
    for ref, table, out in ((dens_ref, wave_ref, dens_out), (green_ref, even_ref, green_out)):
        result = dot3((table[0], table[1]), split(ref[...]), ((1,), (1,)))
        for tile in range(tiles):
            rows = pl.ds(step * tiles + tile, result.shape[0], stride=groups)
            out[rows, :] = result[:, tile * 128 : (tile + 1) * 128]


def plane_kernel(sizes, dens_ref, green_ref, y_ref, ky_ref, x_ref, kx_ref, xi_ref, yi_ref, out_ref):
    nrow, ncol, groups, per, width = sizes
    rows = nrow * groups

    def plane(block):
        block = block.reshape(nrow, ncol, groups, 128)
        return jnp.concatenate(
            [
                jnp.concatenate(
                    [
                        block[:, c, :, h * width : (h + 1) * width].reshape(rows, width)
                        for c in range(ncol)
                    ],
                    axis=1,
                )
                for h in range(per)
            ],
            axis=0,
        )

    def pair(ref):
        return ref[0], ref[1]

    green = dot3(split(plane(green_ref[:, 0])), pair(ky_ref))
    green = dot3(pair(kx_ref), split(green))
    green = jnp.concatenate([green, green], axis=1)
    green = jnp.concatenate([green, green], axis=0)
    for part in range(2):
        value = dot3(split(plane(dens_ref[:, part, 0])), pair(y_ref))
        value = dot3(pair(x_ref), split(value)) * green
        value = dot3(pair(xi_ref), split(value))
        value = dot3(split(value), pair(yi_ref))
        blocks = [
            value[h * rows : (h + 1) * rows].reshape(nrow, groups, ncol * width)
            for h in range(per)
        ]
        for c in range(ncol):
            piece = jnp.concatenate([b[:, :, c * width : (c + 1) * width] for b in blocks], axis=2)
            for r in range(nrow):
                out_ref[r * ncol + c, part, 0] = piece[r]


def inverse_z_kernel(groups, in_ref, wave_ref, out_ref):
    step = pl.program_id(0)
    tiles = out_ref.shape[0] // 128
    count = in_ref.shape[0] // groups
    for tile in range(tiles):
        value = in_ref[pl.ds(step * tiles + tile, count, stride=groups), :]
        result = dot3((wave_ref[0], wave_ref[1]), split(value))
        out_ref[pl.ds(tile * 128, 128), :] = result.T


def whole(array):
    zeros = (0,) * len(array.shape)
    return pl.BlockSpec(array.shape, lambda i: zeros)


def make(mesh):
    nrow, ncol = mesh.shape["row"], mesh.shape["col"]
    ndev = nrow * ncol

    def on_device(density, green_octant):
        xl, width, extent = density.shape
        slots = extent // ndev
        per = 128 // width
        groups = xl // per
        cells = xl * width
        cosine, sine, even = trig(extent)
        waves = np.stack(
            [cosine.reshape(ndev, slots, extent), sine.reshape(ndev, slots, extent)], axis=1
        ).reshape(2 * extent, extent)
        both = np.concatenate([cosine, sine], axis=0)
        order = np.arange(extent).reshape(nrow, groups, per).transpose(2, 0, 1).reshape(-1)
        scale = 1.0 / extent

        params = pltpu.CompilerParams(vmem_limit_bytes=VMEM_BYTES)
        block = min(256, cells)
        z_tables = (halves(waves), halves(even))
        dens, green = pl.pallas_call(
            lambda *refs: forward_z_kernel(groups, *refs),
            grid=(cells // block,),
            in_specs=[pl.BlockSpec((block, extent), lambda i: (i, 0))] * 2
            + [whole(t) for t in z_tables],
            out_specs=[
                pl.BlockSpec((2 * extent * groups, 128), lambda i: (0, 0)),
                pl.BlockSpec((extent * groups, 128), lambda i: (0, 0)),
            ],
            out_shape=[
                jax.ShapeDtypeStruct((2 * extent * groups, 128), F32),
                jax.ShapeDtypeStruct((extent * groups, 128), F32),
            ],
            compiler_params=params,
            name="forward_z",
        )(density.reshape(cells, extent), green_octant.reshape(cells, extent), *z_tables)

        dens = dens.reshape(ndev, 2, slots, groups, 128)
        green = green.reshape(ndev, slots, groups, 128)
        axes = ("row", "col")
        green = lax.all_to_all(green, axes, split_axis=0, concat_axis=0, tiled=True)
        dens = lax.all_to_all(dens, axes, split_axis=0, concat_axis=0, tiled=True)

        tables = (
            halves(both.T),
            halves(even.T),
            halves(both[:, order]),
            halves(even[:, order]),
            halves(both[:, order].T * scale),
            halves(both * scale),
        )
        spec = pl.BlockSpec((ndev, 2, 1, groups, 128), lambda i: (0, 0, i, 0, 0))
        sizes = (nrow, ncol, groups, per, width)
        result = pl.pallas_call(
            lambda *refs: plane_kernel(sizes, *refs),
            grid=(slots,),
            in_specs=[spec, pl.BlockSpec((ndev, 1, groups, 128), lambda i: (0, i, 0, 0))]
            + [whole(t) for t in tables],
            out_specs=spec,
            out_shape=jax.ShapeDtypeStruct(dens.shape, F32),
            compiler_params=params,
            name="planes",
        )(dens, green, *tables)

        result = lax.all_to_all(result, axes, split_axis=0, concat_axis=0, tiled=True)
        back = halves(waves.T * scale)
        out = pl.pallas_call(
            lambda *refs: inverse_z_kernel(groups, *refs),
            grid=(cells // block,),
            in_specs=[
                pl.BlockSpec((2 * extent * groups, 128), lambda i: (0, 0)),
                whole(back),
            ],
            out_specs=pl.BlockSpec((block, extent), lambda i: (i, 0)),
            out_shape=jax.ShapeDtypeStruct((cells, extent), F32),
            compiler_params=params,
            name="inverse_z",
        )(result.reshape(2 * extent * groups, 128), back)
        return out.reshape(xl, width, extent)

    return on_device


def solution(mesh):
    return jax.shard_map(
        make(mesh),
        mesh=mesh,
        in_specs=(P("row", "col", None), P("row", "col", None)),
        out_specs=P("row", "col", None),
        check_vma=False,
    )
```

time: 1020 us -> 304 us (0.30); the launches traced: 1010 us -> 302 us
  local copies, waits for them, and re-layouts: 386 us -> 0.01 us
  matrix products: 246 us -> 0 us
  blocking collectives: 27 us -> 249 us
  other arithmetic: 162 us -> 0 us
  waiting for transfers between devices: 116 us -> 0 us
  starting transfers between devices: 70 us -> 0 us
  Pallas kernels: 0 us -> 53.5 us
    all_to_all x0 -> x3, blocking collectives: none -> 249 us  [the longest x1 97 us: on_device(): lax.all_to_all(result, axes, split_axis=0, concat_axis=0, tiled=True)]
    unnamed x18 -> x0, matrix products: 187 us -> none
    all_to_all x31 -> x0, local copies, waits for them, and re-layouts: 162 us -> none  [the longest x2 20.7 us: on_device(): lax.all_to_all(imaginary, 'col', split_axis=2, concat_axis=1, tiled=True)]
    unnamed x64 -> x2, local copies, waits for them, and re-layouts: 150 us -> 0.01 us
    all_to_all x15 -> x0, waiting for transfers between devices: 116 us -> none  [the longest x1 32.2 us: on_device(): lax.all_to_all(imaginary, 'col', split_axis=2, concat_axis=1, tiled=True)]
    all_to_all x15 -> x0, other arithmetic: 116 us -> none  [the longest x1 14.1 us: on_device(): lax.all_to_all(imaginary, 'row', split_axis=1, concat_axis=0, tiled=True)]
    all_to_all x15 -> x0, starting transfers between devices: 70 us -> none  [the longest x1 6.35 us: on_device(): lax.all_to_all(imaginary, 'col', split_axis=2, concat_axis=1, tiled=True)]
    dot_general x21 -> x0, matrix products: 58.8 us -> none  [contract(): jnp.einsum(pattern, operand, matrix, precision=lax.Precision.HIGHEST, pre...]
  transfers between devices with their start and end apart: 15 -> 0, of which waited for: 6 -> 0; matrix products, arithmetic and copies ran while one was open for 69% -> 0% of each run, Pallas kernels for 0% -> 0%
where the time goes in v1:
time: 304 us; the launch traced here: 302 us
  blocking collectives  249 us (82%)
  Pallas kernels  53.5 us (18%)
    all_to_all x1, blocking collectives, on_device(): lax.all_to_all(result, axes, split_axis=0, concat_axis=0, tiled=True)  97 us
    all_to_all x1, blocking collectives, on_device(): dens = lax.all_to_all(dens, axes, split_axis=0, concat_axis=0, tiled=True)  96.8 us
    all_to_all x1, blocking collectives, on_device(): green = lax.all_to_all(green, axes, split_axis=0, concat_axis=0, tiled=True)  54.8 us
    pallas_call x1, Pallas kernels, on_device(): pl.pallas_call(lambda *refs: plane_kernel(sizes, *refs), grid=(slots,), i...  33.2 us
    pallas_call x1, Pallas kernels, on_device(): pl.pallas_call(lambda *refs: forward_z_kernel(groups, *refs), grid=(cells...  10.6 us
    pallas_call x1, Pallas kernels, on_device(): pl.pallas_call(lambda *refs: inverse_z_kernel(groups, *refs), grid=(cells...  9.69 us

profile of v1, /device:TPU:0, one launch (start us, length us, event | category | flops | bytes accessed | tf_op | source)
XLA Modules:
  0.0 302.2 jit_solution(4688693271832805550)
XLA Ops:
  0.0 10.6 %forward_z.1 = (f32[8192,128]{1,0:T(8,128)}, f32[4096,128]{1,0:T(8,128)}) custom-call(f32[2048,256]{1,0:T(8,128)} %bitcast.8, f32[2048,256]{1,0:T(8,128)} %bitcast.9, bf16[2,512,256]{2,1,0:T(8,128)(2,1)} %constant.18.clone.refs_2_, bf16[2,256,256]{2,1,0:T(8,128)(2,1)} %constant.19.clone.refs_3_), custom_call_target="tpu_custom_call" | custom-call | tf_op jit(solution)/shard_map/forward_z/pallas_call | solution.py:130
  10.6 0.0 copy-start
  10.6 54.8 %all_to_all.15.refs_1_ = f32[32,8,16,128]{3,2,1,0:T(8,128)} all-to-all(f32[32,8,16,128]{3,2,1,0:T(8,128)} %bitcast.10), channel_id=1, replica_groups=mesh['row'=8,'col'=4] {'row','col'}, dimensions={0} | all-to-all | bytes 4194304 | tf_op jit(solution)/shard_map/all_to_all | solution.py:150
  65.4 0.0 copy-done
  65.4 96.8 %all_to_all.16.refs_0_ = f32[32,2,8,16,128]{4,3,2,1,0:T(8,128)} all-to-all(f32[32,2,8,16,128]{4,3,2,1,0:T(8,128)S(1)} %bitcast.7), channel_id=1, replica_groups=mesh['row'=8,'col'=4] {'row','col'}, dimensions={0} | all-to-all | bytes 8388608 | tf_op jit(solution)/shard_map/all_to_all | solution.py:151
  162.2 33.2 %planes.1 = f32[32,2,8,16,128]{4,3,2,1,0:T(8,128)} custom-call(f32[32,2,8,16,128]{4,3,2,1,0:T(8,128)} %all_to_all.16.refs_0_, f32[32,8,16,128]{3,2,1,0:T(8,128)} %all_to_all.15.refs_1_, bf16[2,256,512]{2,1,0:T(8,128)(2,1)} %constant.20.clone.refs_2_, bf16[2,256,256]{2,1,0:T(8,128)(2,1)} %constant.21.clone.refs_3_, ...), custom_call_target="tpu_custom_call" | custom-call | tf_op jit(solution)/shard_map/planes/pallas_call | solution.py:163
  195.5 97.0 %all_to_all.17 = f32[32,2,8,16,128]{4,3,2,1,0:T(8,128)} all-to-all(f32[32,2,8,16,128]{4,3,2,1,0:T(8,128)} %planes.1), channel_id=1, replica_groups=mesh['row'=8,'col'=4] {'row','col'}, dimensions={0} | all-to-all | bytes 8388608 | tf_op jit(solution)/shard_map/all_to_all | solution.py:174
  292.5 9.7 %inverse_z.1 = f32[2048,256]{1,0:T(8,128)} custom-call(f32[8192,128]{1,0:T(8,128)} %bitcast.6, bf16[2,256,512]{2,1,0:T(8,128)(2,1)} %constant.26.clone.refs_1_), custom_call_target="tpu_custom_call" | custom-call | tf_op jit(solution)/shard_map/inverse_z/pallas_call | solution.py:176
Async XLA Ops:
  10.6 54.8 %copy-start = (f32[8192,128]{1,0:T(8,128)S(1)}, f32[8192,128]{1,0:T(8,128)}, u32[]{:S(2)}) copy-start(f32[8192,128]{1,0:T(8,128)} %get-tuple-element.7) | copy-start | bytes 12582916

commit v2 on v1

v2 whole, which is shorter than its diff:
```python
import jax
import jax.numpy as jnp
import numpy as np
from jax import lax
from jax.experimental import pallas as pl
from jax.experimental.pallas import tpu as pltpu
from jax.sharding import PartitionSpec as P

F32 = jnp.float32
BF16 = jnp.bfloat16
VMEM_BYTES = 60 * 1024 * 1024


def trig(extent):
    k = np.arange(extent)[:, None]
    n = np.arange(extent)[None, :]
    phase = ((2 * k + 1) * n) % (4 * extent)
    angle = 2.0 * np.pi * phase / (4 * extent)
    weight = np.where(n == 0, 1.0, 2.0)
    return np.cos(angle), np.sin(angle), weight * np.cos(angle)


def halves(table):
    table = np.asarray(table, np.float32)
    high = table.astype(BF16)
    low = (table - high.astype(np.float32)).astype(BF16)
    return jnp.asarray(np.stack([high, low]))


def split(value):
    high = value.astype(BF16)
    return high, (value - high.astype(F32)).astype(BF16)


def dot3(left, right, dims=((1,), (0,))):
    def one(a, b):
        return lax.dot_general(a, b, (dims, ((), ())), preferred_element_type=F32)

    return one(left[0], right[0]) + (one(left[0], right[1]) + one(left[1], right[0]))


def fused_kernel(sizes, dens_ref, green_ref, wave_ref, even_ref, y_ref, ky_ref, x_ref, kx_ref,
                 xi_ref, yi_ref, back_ref, out_ref, dens_two, green_two, send, recv, bsend, brecv,
                 total, send_sem, recv_sem, bsend_sem, brecv_sem):
    nrow, ncol, groups, per, width, chunks, each, parts = sizes
    ndev = nrow * ncol
    rows = nrow * groups
    cells = dens_ref.shape[0]
    me = lax.axis_index("row") * ncol + lax.axis_index("col")
    size, bsize = each * 3 * groups, each * 2 * groups

    def other(step):
        target = lax.rem(me + step, ndev)
        return target, (lax.div(target, ncol), lax.rem(target, ncol))

    barrier = pltpu.get_barrier_semaphore()

    def greet(step, carry):
        pl.semaphore_signal(
            barrier, inc=1, device_id=other(step)[1], device_id_type=pl.DeviceIdType.MESH
        )
        return carry

    lax.fori_loop(1, ndev, greet, 0)

    def pair(ref):
        return ref[0], ref[1]

    def block(ref, chunk, owner, length):
        start = pl.multiple_of((chunk * ndev + owner) * length, 8)
        return ref.at[pl.ds(start, length), :]

    def spread(source, target, length, chunk, out_sem, in_sem):
        def one(step, carry):
            owner, device = other(step)
            pltpu.make_async_remote_copy(
                src_ref=block(source, chunk, owner, length),
                dst_ref=block(target, chunk, me, length),
                send_sem=out_sem.at[chunk],
                recv_sem=in_sem.at[chunk],
                device_id=device,
                device_id_type=pl.DeviceIdType.MESH,
            ).start()
            return carry

        lax.fori_loop(1, ndev, one, 0)
        block(target, chunk, me, length)[...] = block(source, chunk, me, length)[...]

    def landed(ref, length, chunk, sem):
        start = pl.multiple_of(chunk * ndev * length, 8)
        view = ref.at[pl.ds(start, (ndev - 1) * length), :]
        pltpu.make_async_copy(view, view, sem.at[chunk]).wait()

    for ref, two in ((dens_ref, dens_two), (green_ref, green_two)):
        high, low = split(ref[...])
        two[0] = high
        two[1] = low

    lines = ndev * each
    step_cells = min(256, cells)

    def transform(chunk):
        for two, table, first, count in (
            (dens_two, wave_ref, 0, 2),
            (green_two, even_ref, 2, 1),
        ):
            left = (table[0, chunk], table[1, chunk])
            for begin in range(0, cells, step_cells):
                right = (two[0, begin : begin + step_cells], two[1, begin : begin + step_cells])
                result = dot3(left, right, ((1,), (1,)))
                for part in range(count):
                    for tile in range(step_cells // 128):
                        group = begin // 128 + tile
                        start = chunk * ndev * size + (first + part) * groups + group
                        send[pl.ds(start, lines, stride=3 * groups), :] = result[
                            part * lines : (part + 1) * lines, tile * 128 : (tile + 1) * 128
                        ]

    transform(0)
    pl.semaphore_wait(barrier, ndev - 1)
    spread(send, recv, size, 0, send_sem, recv_sem)

    def forward(chunk, carry):
        transform(chunk)
        spread(send, recv, size, chunk, send_sem, recv_sem)
        return carry

    lax.fori_loop(1, chunks, forward, 0)

    def planes(chunk, carry):
        landed(recv, size, chunk, recv_sem)

        def load(slot, part):
            def piece(r, c):
                start = ((chunk * ndev + r * ncol + c) * each + slot) * 3 * groups + part * groups
                return recv[pl.ds(start, groups), :]

            columns = [
                jnp.concatenate([piece(r, c) for r in range(nrow)], axis=0) for c in range(ncol)
            ]
            return jnp.concatenate(
                [
                    jnp.concatenate([v[:, h * width : (h + 1) * width] for v in columns], axis=1)
                    for h in range(per)
                ],
                axis=0,
            )

        def one_slot(slot, inner):
            green = dot3(split(load(slot, 2)), pair(ky_ref))
            green = dot3(pair(kx_ref), split(green))
            green = jnp.concatenate([green, green], axis=1)
            green = jnp.concatenate([green, green], axis=0)
            for part in range(2):
                value = dot3(split(load(slot, part)), pair(y_ref))
                value = dot3(pair(x_ref), split(value)) * green
                value = dot3(pair(xi_ref), split(value))
                value = dot3(split(value), pair(yi_ref))
                for c in range(ncol):
                    piece = jnp.concatenate(
                        [
                            value[h * rows : (h + 1) * rows, c * width : (c + 1) * width]
                            for h in range(per)
                        ],
                        axis=1,
                    )
                    for r in range(nrow):
                        start = ((chunk * ndev + r * ncol + c) * each + slot) * 2 * groups
                        start = start + part * groups
                        bsend[pl.ds(start, groups), :] = piece[r * groups : (r + 1) * groups]
            return inner

        lax.fori_loop(0, each, one_slot, 0)
        spread(bsend, brecv, bsize, chunk, bsend_sem, brecv_sem)
        return carry

    lax.fori_loop(0, chunks, planes, 0)

    depth = 2 * lines * chunks // parts
    for half in range(parts):
        for chunk in range(half * chunks // parts, (half + 1) * chunks // parts):
            landed(brecv, bsize, chunk, brecv_sem)
        for group in range(groups):
            value = brecv[pl.ds(half * depth * groups + group, depth, stride=groups), :]
            table = (back_ref[0, half], back_ref[1, half])
            result = dot3(table, split(value))
            if half > 0:
                result = result + total[:, group * 128 : (group + 1) * 128]
            if half < parts - 1:
                total[:, group * 128 : (group + 1) * 128] = result
            else:
                out_ref[pl.ds(group * 128, 128), :] = result.T

    def finish(chunk, carry):
        landed(send, size, chunk, send_sem)
        landed(bsend, bsize, chunk, bsend_sem)
        return carry

    lax.fori_loop(0, chunks, finish, 0)


def make(mesh):
    nrow, ncol = mesh.shape["row"], mesh.shape["col"]
    ndev = nrow * ncol

    def on_device(density, green_octant):
        xl, width, extent = density.shape
        slots = extent // ndev
        per = 128 // width
        groups = xl // per
        cells = xl * width
        each = min(2, slots)
        chunks = slots // each
        parts = 2 if chunks % 2 == 0 else 1
        cosine, sine, even = trig(extent)

        def chunked(table):
            return table.reshape(ndev, chunks, each, extent).transpose(1, 0, 2, 3)

        lines = ndev * each
        waves = np.stack([chunked(cosine), chunked(sine)], axis=1).reshape(
            chunks, 2 * lines, extent
        )
        evens = chunked(even).reshape(chunks, lines, extent)
        back = np.stack([chunked(cosine), chunked(sine)], axis=3).reshape(parts, -1, extent)
        back = back.transpose(0, 2, 1)
        both = np.concatenate([cosine, sine], axis=0)
        order = np.arange(extent).reshape(nrow, groups, per).transpose(2, 0, 1).reshape(-1)
        scale = 1.0 / extent
        tables = (
            halves(waves),
            halves(evens),
            halves(both.T),
            halves(even.T),
            halves(both[:, order]),
            halves(even[:, order]),
            halves(both[:, order].T * scale),
            halves(both * scale),
            halves(back * scale),
        )
        operands = (
            density.reshape(cells, extent),
            green_octant.reshape(cells, extent),
        ) + tables
        size, bsize = each * 3 * groups, each * 2 * groups
        sizes = (nrow, ncol, groups, per, width, chunks, each, parts)
        out = pl.pallas_call(
            lambda *refs: fused_kernel(sizes, *refs),
            in_specs=[pl.BlockSpec(memory_space=pltpu.VMEM)] * len(operands),
            out_specs=pl.BlockSpec(memory_space=pltpu.VMEM),
            out_shape=jax.ShapeDtypeStruct((cells, extent), F32),
            scratch_shapes=[
                pltpu.VMEM((2, cells, extent), BF16),
                pltpu.VMEM((2, cells, extent), BF16),
                pltpu.VMEM((chunks * ndev * size, 128), F32),
                pltpu.VMEM((chunks * ndev * size, 128), F32),
                pltpu.VMEM((chunks * ndev * bsize, 128), F32),
                pltpu.VMEM((chunks * ndev * bsize, 128), F32),
                pltpu.VMEM((extent, cells), F32),
            ]
            + [pltpu.SemaphoreType.DMA((chunks,))] * 4,
            compiler_params=pltpu.CompilerParams(
                vmem_limit_bytes=VMEM_BYTES, collective_id=0, has_side_effects=True
            ),
            name="fused",
        )(*operands)
        return out.reshape(xl, width, extent)

    return on_device


def solution(mesh):
    return jax.shard_map(
        make(mesh),
        mesh=mesh,
        in_specs=(P("row", "col", None), P("row", "col", None)),
        out_specs=P("row", "col", None),
        check_vma=False,
    )
```

time: 304 us -> 243 us (0.80)
  blocking collectives: 249 us -> 0 us
  Pallas kernels: 53.5 us -> 240 us
  local copies, waits for them, and re-layouts: 0.01 us -> 3.13 us
    all_to_all x3 -> x0, blocking collectives: 249 us -> none  [the longest x1 97 us: on_device(): lax.all_to_all(result, axes, split_axis=0, concat_axis=0, tiled=True)]
    pallas_call x3 -> x1, Pallas kernels: 53.5 us -> 240 us  [on_device(): pl.pallas_call(lambda *refs: fused_kernel(sizes, *refs), in_specs=[pl.Blo...]
    unnamed x2 -> x1, local copies, waits for them, and re-layouts: 0.01 us -> 3.13 us
where the time goes in v2:
time: 243 us
  Pallas kernels  240 us (99%)
  local copies, waits for them, and re-layouts  3.13 us (1%)
    pallas_call x1, Pallas kernels, on_device(): pl.pallas_call(lambda *refs: fused_kernel(sizes, *refs), in_specs=[pl.Blo...  240 us

profile of v2, /device:TPU:0, one launch (start us, length us, event | category | flops | bytes accessed | tf_op | source)
XLA Modules:
  0.0 242.8 jit_solution(17761680131898560996)
XLA Ops:
  0.0 239.7 %fused.1 = f32[2048,256]{1,0:T(8,128)} custom-call(f32[2048,256]{1,0:T(8,128)} %bitcast.4, f32[2048,256]{1,0:T(8,128)} %bitcast.5, bf16[2,4,128,256]{3,2,1,0:T(8,128)(2,1)} %constant.18.clone.refs_2_, bf16[2,4,64,256]{3,2,1,0:T(8,128)(2,1)} %constant.19.clone.refs_3_, bf16[2,256,512]{2,1,0:T(8,128)(2,1)} %constant.20.clone.refs_4_, ...), custom_call_target="tpu_custom_call" | custom-call | tf_op jit(solution)/shard_map/fused/pallas_call | solution.py:247
  239.7 3.1 %copy.13 = f32[32,64,256]{2,1,0:T(8,128)} copy(f32[32,64,256]{2,1,0:T(8,128)} %bitcast.3) | data formatting | bytes 4194304
